TPU v7x, 32 devices: a whole 2x2x4 slice. The times are simulated.
32 devices in a mesh: shard: 8 (over z, y), tp: 4 (over x, core).
Axes of the slice: x: 2, y: 2, z: 4, core: 2. Of those that a mesh axis runs over, the one named last changes fastest.
Arguments:
- gradient: bfloat16 [4096, 16384], P('shard', 'tp'), may hold values from -2 to 2
- table: int32 [256, 3], replicated, may hold values from 0 to 31, as said below
- left_stat: bfloat16 [384, 512, 512], P(('shard', 'tp')), as said below
- right_stat: bfloat16 [384, 512, 512], P(('shard', 'tp')), as said below
- left_basis: bfloat16 [384, 512, 512], P(('shard', 'tp')), may hold values from -0.25 to 0.25
- right_basis: bfloat16 [384, 512, 512], P(('shard', 'tp')), may hold values from -0.25 to 0.25
- moment: bfloat16 [384, 512, 512], P(('shard', 'tp')), may hold values from -2 to 2
- second: float32 [384, 512, 512], P(('shard', 'tp')), may hold values from 0.02 to 0.2
Outputs:
- update: bfloat16 [4096, 16384], P('shard', 'tp')
- new_left: bfloat16 [384, 512, 512], P(('shard', 'tp'))
- new_right: bfloat16 [384, 512, 512], P(('shard', 'tp'))
- new_moment: bfloat16 [384, 512, 512], P(('shard', 'tp'))
- new_second: float32 [384, 512, 512], P(('shard', 'tp'))
Inputs may be any that keep to these rules, and one draw needn't show every extreme that they name: `table`: column 0 is a block row below 8, column 1 a block column below 32, column 2 an owner device below 32; every block appears in exactly one row; each device owns between 4 and 12 blocks, and some device owns exactly 12. `left_stat`: Symmetric. `right_stat`: Symmetric.
All inputs are finite; a program needn't handle non-finite values.
Results may differ from a plain program's by a relative error of at most 0.0085.
Values may be sent and summed in bfloat16 or wider, within the bound.
A program may use at most 192 MiB of HBM per device.

v0:
```python
import functools

import jax
import jax.numpy as jnp
from jax import lax
from jax.experimental import pallas as pl
from jax.experimental.pallas import tpu as pltpu
from jax.sharding import PartitionSpec as P

beta_moment = 0.9
beta_second = 0.95
beta_stats = 0.95
epsilon = 1e-08
AXES = ("shard", "tp")


def slot_table(table, slots):
    owners = table[:, 2]
    count = owners.shape[0]
    order = jnp.arange(count, dtype=jnp.int32)
    earlier = (owners[None, :] == owners[:, None]) & (order[None, :] < order[:, None])
    slot_rank = jnp.sum(earlier.astype(jnp.int32), axis=1)
    return owners * slots + slot_rank


def exchange(array):
    return lax.all_to_all(array, AXES, split_axis=0, concat_axis=0, tiled=True)


def dot(a, b, dims):
    return lax.dot_general(a, b, (dims, ((), ())), preferred_element_type=jnp.float32)


def pack_kernel(group, slots, first, count, halves, tp_count, side, src_ref, col_ref, in_ref, out_ref):
    base = pl.program_id(0) * group

    def device(d, carry):
        for k in range(count):
            entry = (base + d) * slots + first + k
            src = src_ref[entry]
            col = pl.multiple_of(col_ref[entry] * side, side)
            for h in range(halves):
                out_ref[d, k, h] = in_ref[src + h * tp_count, :, pl.ds(col, side)]
        return carry

    lax.fori_loop(0, group, device, 0)


def pack(received, src, col, slots, first, count, halves, tp_count, side):
    dev_count, rows, cols = received.shape
    group = 4 if dev_count % 4 == 0 else 1
    return pl.pallas_call(
        functools.partial(pack_kernel, group, slots, first, count, halves, tp_count, side),
        grid_spec=pltpu.PrefetchScalarGridSpec(
            num_scalar_prefetch=2,
            grid=(dev_count // group,),
            in_specs=[pl.BlockSpec((dev_count, rows, cols), lambda i, *_: (0, 0, 0))],
            out_specs=pl.BlockSpec((group, count, halves, rows, side), lambda i, *_: (i, 0, 0, 0, 0)),
        ),
        out_shape=jax.ShapeDtypeStruct((dev_count, count, halves, rows, side), received.dtype),
        cost_estimate=pl.CostEstimate(flops=0, bytes_accessed=received.size * 6, transcendentals=0),
    )(src, col, received)


def unpack_kernel(group, firsts, halves, tp_count, cols_per_dev, side, own_ref, slot_ref, *refs):
    out_ref = refs[-1]
    base = pl.program_id(0) * group

    def device(d, carry):
        dev = base + d
        shard = dev // tp_count
        half = shard % halves
        place = (shard // halves * tp_count + dev % tp_count) * cols_per_dev
        for c in range(cols_per_dev):
            owner = own_ref[place + c]
            slot = slot_ref[place + c]
            value = refs[0][owner, jnp.minimum(slot, refs[0].shape[1] - 1), half]
            for ref, first in zip(refs[1:-1], firsts[1:]):
                inner = jnp.clip(slot - first, 0, ref.shape[1] - 1)
                value = jnp.where(slot >= first, ref[owner, inner, half], value)
            out_ref[d, :, c * side : (c + 1) * side] = value
        return carry

    lax.fori_loop(0, group, device, 0)


def unpack(chunks, firsts, own, slot, tp_count, cols_per_dev):
    dev_count, _, halves, rows, side = chunks[0].shape
    group = 4 if dev_count % 4 == 0 else 1
    cols = cols_per_dev * side
    return pl.pallas_call(
        functools.partial(unpack_kernel, group, firsts, halves, tp_count, cols_per_dev, side),
        grid_spec=pltpu.PrefetchScalarGridSpec(
            num_scalar_prefetch=2,
            grid=(dev_count // group,),
            in_specs=[pl.BlockSpec(c.shape, lambda i, *_: (0, 0, 0, 0, 0)) for c in chunks],
            out_specs=pl.BlockSpec((group, rows, cols), lambda i, *_: (i, 0, 0)),
        ),
        out_shape=jax.ShapeDtypeStruct((dev_count, rows, cols), chunks[0].dtype),
        cost_estimate=pl.CostEstimate(flops=0, bytes_accessed=dev_count * rows * cols * 5, transcendentals=0),
    )(own, slot, *chunks)


def slot_kernel(first, packed, mine_ref, x_ref, left, right, left_q, right_q, moment, second, *refs):
    out_ref, left_o, right_o, moment_o, second_o = refs[-5:]
    side = left.shape[-1]
    used = mine_ref[first + pl.program_id(0)] > 0

    @pl.when(used)
    def _():
        if packed:
            halves = x_ref.shape[2]
            parts = [x_ref[:, 0, h].reshape(side // halves, side) for h in range(halves)]
            grad = parts[0] if halves == 1 else jnp.concatenate(parts, axis=0)
        else:
            grad = x_ref[0]
        ql = left_q[0]
        qr = right_q[0]
        first_new = (
            beta_moment * moment[0].astype(jnp.float32)
            + (1.0 - beta_moment) * grad.astype(jnp.float32)
        ).astype(jnp.bfloat16)
        moment_o[0] = first_new
        left_grad = dot(ql, grad, ((0,), (0,))).astype(jnp.bfloat16)
        rotated = dot(left_grad, qr, ((1,), (0,)))
        squares_new = beta_second * second[0] + (1.0 - beta_second) * rotated * rotated
        second_o[0] = squares_new
        left_first = dot(ql, first_new, ((0,), (0,))).astype(jnp.bfloat16)
        first_rot = dot(left_first, qr, ((1,), (0,)))
        scaled = (first_rot / (jnp.sqrt(squares_new) + epsilon)).astype(jnp.bfloat16)
        back = dot(ql, scaled, ((1,), (0,))).astype(jnp.bfloat16)
        result = dot(back, qr, ((1,), (1,))).astype(jnp.bfloat16)
        if packed:
            halves = x_ref.shape[2]
            step = side // halves
            for h in range(halves):
                out_ref[:, 0, h] = result[h * step : (h + 1) * step].reshape(
                    x_ref.shape[0], x_ref.shape[3], side
                )
        else:
            out_ref[0] = result
        left_o[0] = (
            beta_stats * left[0].astype(jnp.float32)
            + (1.0 - beta_stats) * dot(grad, grad, ((1,), (1,)))
        ).astype(jnp.bfloat16)
        right_o[0] = (
            beta_stats * right[0].astype(jnp.float32)
            + (1.0 - beta_stats) * dot(grad, grad, ((0,), (0,)))
        ).astype(jnp.bfloat16)

    @pl.when(jnp.logical_not(used))
    def _():
        out_ref[...] = jnp.zeros_like(out_ref)
        left_o[...] = left[...]
        right_o[...] = right[...]
        moment_o[...] = moment[...]
        second_o[...] = second[...]


def precondition(x, mine, states, done, first, packed):
    left = states[0]
    slots, side, _ = left.shape
    if packed:
        dev_count, count, halves, rows, _ = x.shape
        x_spec = pl.BlockSpec((dev_count, 1, halves, rows, side), lambda i, *_: (0, i, 0, 0, 0))
    else:
        count = x.shape[0]
        x_spec = pl.BlockSpec((1, side, side), lambda i, *_: (i, 0, 0))
    state_spec = pl.BlockSpec((1, side, side), lambda i, *_: (first + i, 0, 0))
    done = list(done)
    kept = [jax.ShapeDtypeStruct(states[k].shape, states[k].dtype) for k in (0, 1, 4, 5)]
    return pl.pallas_call(
        functools.partial(slot_kernel, first, packed),
        grid_spec=pltpu.PrefetchScalarGridSpec(
            num_scalar_prefetch=1,
            grid=(count,),
            in_specs=[x_spec] + [state_spec] * 6 + [pl.BlockSpec(memory_space=pl.ANY)] * len(done),
            out_specs=[x_spec] + [state_spec] * 4,
        ),
        out_shape=[jax.ShapeDtypeStruct(x.shape, x.dtype)] + kept,
        input_output_aliases={8 + k: 1 + k for k in range(len(done))},
        cost_estimate=pl.CostEstimate(
            flops=count * 16 * side**3,
            bytes_accessed=count * side * side * 26,
            transcendentals=count * side * side,
        ),
    )(mine, x, *states, *done)


def shards(gradient, table, left_stat, right_stat, left_basis, right_basis, moment, second):
    shard_count = lax.axis_size("shard")
    tp_count = lax.axis_size("tp")
    dev_count = shard_count * tp_count
    row_dev, col_dev = gradient.shape
    slots = left_stat.shape[0]
    side = left_stat.shape[1]
    halves = side // row_dev
    cols_per_dev = col_dev // side
    block_cols = tp_count * cols_per_dev
    rows = row_dev // dev_count
    packed = rows % 16 == 0
    received = exchange(gradient.reshape(dev_count, rows, col_dev))

    state_row = slot_table(table, slots)
    block_id = table[:, 0] * block_cols + table[:, 1]
    targets = jnp.arange(dev_count * slots, dtype=jnp.int32)
    matches = (state_row[None, :] == targets[:, None]).astype(jnp.int32)
    send_id = jnp.sum(matches * block_id[None, :], axis=1)
    filled = jnp.sum(matches, axis=1)
    send_col = send_id % block_cols
    src = (send_id // block_cols) * halves * tp_count + send_col // cols_per_dev
    col = send_col % cols_per_dev
    myself = lax.axis_index(AXES)
    mine = lax.dynamic_slice_in_dim(filled, myself * slots, slots)
    positions = jnp.arange(table.shape[0], dtype=jnp.int32)
    block_match = (block_id[None, :] == positions[:, None]).astype(jnp.int32)
    slot_of_block = jnp.sum(block_match * state_row[None, :], axis=1)
    own = slot_of_block // slots
    slot = slot_of_block % slots

    half = (slots + 1) // 2
    chunks = [(0, half), (half, slots - half)] if slots > 1 else [(0, slots)]
    states = (left_stat, right_stat, left_basis, right_basis, moment, second)
    tiles = received.reshape(dev_count, rows, cols_per_dev, side)
    half_index = jnp.arange(halves, dtype=jnp.int32)
    inbox = []
    for first, count in chunks:
        if packed:
            out = pack(received, src, col, slots, first, count, halves, tp_count, side)
        else:
            src_c = src.reshape(dev_count, slots)[:, first : first + count]
            col_c = col.reshape(dev_count, slots)[:, first : first + count]
            out = tiles[src_c[:, :, None] + half_index * tp_count, :, col_c[:, :, None]]
        inbox.append(exchange(out))
    done = ()
    returned = []
    for x, (first, count) in zip(inbox, chunks):
        if not packed:
            x = x.transpose(1, 2, 0, 3, 4).reshape(count, side, side)
        update, *done = precondition(x, mine, states, done, first, packed)
        if not packed:
            update = update.reshape(count, halves, dev_count, rows, side).transpose(2, 0, 1, 3, 4)
        returned.append(exchange(update))
    if packed:
        outbox = unpack(returned, tuple(f for f, _ in chunks), own, slot, tp_count, cols_per_dev)
    else:
        back = jnp.concatenate(returned, axis=1)
        dev = jnp.arange(dev_count, dtype=jnp.int32)[:, None]
        place = (dev // tp_count // halves * tp_count + dev % tp_count) * cols_per_dev
        place = place + jnp.arange(cols_per_dev, dtype=jnp.int32)[None, :]
        picked = back[own[place], slot[place], dev // tp_count % halves]
        outbox = picked.transpose(0, 2, 1, 3).reshape(dev_count, rows, col_dev)
    update = exchange(outbox).reshape(row_dev, col_dev)
    new_left, new_right, new_moment, new_second = done
    return (update, new_left, new_right, new_moment, new_second)


def solution(mesh):
    state = P(AXES, None, None)
    in_specs = (P("shard", "tp"), P()) + (state,) * 6
    out_specs = (P("shard", "tp"),) + (state,) * 4
    return jax.shard_map(shards, mesh=mesh, in_specs=in_specs, out_specs=out_specs, check_vma=False)
```

profile of v0, /device:TPU:11, one launch (start us, length us, event | category | flops | bytes accessed | tf_op | source)
XLA Modules:
  0.0 518.8 jit_solution(12106552861633704672)
XLA Ops:
  0.6 0.0 copy-start.3
  0.6 6.4 %all-to-all-start = ((bf16[32,16,4096]{2,1,0:T(8,128)(2,1)}), bf16[32,16,4096]{2,1,0:T(8,128)(2,1)}, u32[]{:S(2)}, u32[]{:S(2)}) async-start(bf16[32,16,4096]{2,1,0:T(8,128)(2,1)} %bitcast.5), calls=%async_computation | async-start | bytes 8388608 | tf_op jit(solution)/shard_map/all_to_all | solution.py:27
  7.0 0.0 copy-done.3
  7.0 0.2 convert_reduce_fusion.1
  7.2 0.2 select_reduce_fusion
  7.4 0.6 add_select_fusion
  8.0 90.1 %all-to-all-done.in_ref = bf16[32,16,4096]{2,1,0:T(8,128)(2,1)} async-done(((bf16[32,16,4096]{2,1,0:T(8,128)(2,1)}), bf16[32,16,4096]{2,1,0:T(8,128)(2,1)}, u32[]{:S(2)}, u32[]{:S(2)}) %all-to-all-start) | async-done | bytes 4194336 | tf_op jit(solution)/shard_map/all_to_all | solution.py:27
  98.2 6.3 %shard_map.119 = bf16[32,6,1,16,512]{4,3,2,1,0:T(8,128)(2,1)} custom-call(s32[384]{0:T(512)} %get-tuple-element.30.src_ref, s32[384]{0:T(512)} %get-tuple-element.29.col_ref, bf16[32,16,4096]{2,1,0:T(8,128)(2,1)} %all-to-all-done.in_ref), custom_call_target="tpu_custom_call" | custom-call | bytes 12582912 | tf_op jit(solution)/shard_map/pallas_call | solution.py:52
  104.5 6.7 %all-to-all-start.1 = ((bf16[32,6,1,16,512]{4,3,2,1,0:T(8,128)(2,1)}), bf16[32,6,1,16,512]{4,3,2,1,0:T(8,128)(2,1)S(1)}, u32[]{:S(2)}, u32[]{:S(2)}) async-start(bf16[32,6,1,16,512]{4,3,2,1,0:T(8,128)(2,1)} %shard_map.119), calls=%async_computation.1 | async-start | bytes 6291456 | tf_op jit(solution)/shard_map/all_to_all | solution.py:27
  111.2 6.3 %shard_map.121 = bf16[32,6,1,16,512]{4,3,2,1,0:T(8,128)(2,1)} custom-call(s32[384]{0:T(512)} %get-tuple-element.30.src_ref, s32[384]{0:T(512)} %get-tuple-element.29.col_ref, bf16[32,16,4096]{2,1,0:T(8,128)(2,1)} %all-to-all-done.in_ref), custom_call_target="tpu_custom_call" | custom-call | bytes 12582912 | tf_op jit(solution)/shard_map/pallas_call | solution.py:52
  117.5 62.8 %all-to-all-done.1.x_ref = bf16[32,6,1,16,512]{4,3,2,1,0:T(8,128)(2,1)S(1)} async-done(((bf16[32,6,1,16,512]{4,3,2,1,0:T(8,128)(2,1)}), bf16[32,6,1,16,512]{4,3,2,1,0:T(8,128)(2,1)S(1)}, u32[]{:S(2)}, u32[]{:S(2)}) %all-to-all-start.1) | async-done | bytes 3145760 | tf_op jit(solution)/shard_map/all_to_all | solution.py:27
  180.3 0.0 copy-start.2
  180.3 1.7 copy-done.2
  182.0 6.3 %all-to-all-start.3 = ((bf16[32,6,1,16,512]{4,3,2,1,0:T(8,128)(2,1)}), bf16[32,6,1,16,512]{4,3,2,1,0:T(8,128)(2,1)S(1)}, u32[]{:S(2)}, u32[]{:S(2)}) async-start(bf16[32,6,1,16,512]{4,3,2,1,0:T(8,128)(2,1)} %shard_map.121), calls=%async_computation.3 | async-start | bytes 6291456 | tf_op jit(solution)/shard_map/all_to_all | solution.py:27
  188.3 0.6 dynamic_slice.3.mine_ref
  188.9 21.9 %shard_map.120 = (bf16[32,6,1,16,512]{4,3,2,1,0:T(8,128)(2,1)}, bf16[12,512,512]{2,1,0:T(8,128)(2,1)}, bf16[12,512,512]{2,1,0:T(8,128)(2,1)}, bf16[12,512,512]{2,1,0:T(8,128)(2,1)}, f32[12,512,512]{2,1,0:T(8,128)}) custom-call(s32[12]{0:T(128)} %dynamic_slice.3.mine_ref, bf16[32,6,1,16,512]{4,3,2,1,0:T(8,128)(2,1)} %copy-done.2, bf16[12,512,512]{2,1,0:T(8,128)(2,1)} %left.3, ...), custom_call_target="tpu_custom_call" | custom-call | flops 12884901888 | bytes 40894464 | tf_op jit(solution)/shard_map/pallas_call | solution.py:172
  210.8 46.5 %all-to-all-done.3.x_ref = bf16[32,6,1,16,512]{4,3,2,1,0:T(8,128)(2,1)S(1)} async-done(((bf16[32,6,1,16,512]{4,3,2,1,0:T(8,128)(2,1)}), bf16[32,6,1,16,512]{4,3,2,1,0:T(8,128)(2,1)S(1)}, u32[]{:S(2)}, u32[]{:S(2)}) %all-to-all-start.3) | async-done | bytes 3145760 | tf_op jit(solution)/shard_map/all_to_all | solution.py:27
  257.3 0.0 copy-start
  257.3 6.3 %all-to-all-start.2 = ((bf16[32,6,1,16,512]{4,3,2,1,0:T(8,128)(2,1)}), bf16[32,6,1,16,512]{4,3,2,1,0:T(8,128)(2,1)}, u32[]{:S(2)}, u32[]{:S(2)}) async-start(bf16[32,6,1,16,512]{4,3,2,1,0:T(8,128)(2,1)} %get-tuple-element.15), calls=%async_computation.2 | async-start | bytes 6291456 | tf_op jit(solution)/shard_map/all_to_all | solution.py:27
  263.7 0.0 copy-done
  263.7 20.6 %shard_map.122 = (bf16[32,6,1,16,512]{4,3,2,1,0:T(8,128)(2,1)}, bf16[12,512,512]{2,1,0:T(8,128)(2,1)}, bf16[12,512,512]{2,1,0:T(8,128)(2,1)}, bf16[12,512,512]{2,1,0:T(8,128)(2,1)}, f32[12,512,512]{2,1,0:T(8,128)}) custom-call(s32[12]{0:T(128)} %dynamic_slice.3.mine_ref, ...), custom_call_target="tpu_custom_call", output_to_operand_aliasing={{1}: (8, {}), {2}: (9, {}), {3}: (10, {}), {4}: (11, {})} | custom-call | flops 12884901888 | bytes 40894464 | tf_op jit(solution)/shard_map/pallas_call | solution.py:172
  284.3 48.5 %all-to-all-done.2.refs_0_ = bf16[32,6,1,16,512]{4,3,2,1,0:T(8,128)(2,1)} async-done(((bf16[32,6,1,16,512]{4,3,2,1,0:T(8,128)(2,1)}), bf16[32,6,1,16,512]{4,3,2,1,0:T(8,128)(2,1)}, u32[]{:S(2)}, u32[]{:S(2)}) %all-to-all-start.2) | async-done | bytes 3145760 | tf_op jit(solution)/shard_map/all_to_all | solution.py:27
  332.8 6.3 %all-to-all-start.4 = ((bf16[32,6,1,16,512]{4,3,2,1,0:T(8,128)(2,1)}), bf16[32,6,1,16,512]{4,3,2,1,0:T(8,128)(2,1)S(1)}, u32[]{:S(2)}, u32[]{:S(2)}) async-start(bf16[32,6,1,16,512]{4,3,2,1,0:T(8,128)(2,1)} %get-tuple-element.20), calls=%async_computation.4 | async-start | bytes 6291456 | tf_op jit(solution)/shard_map/all_to_all | solution.py:27
  339.1 0.1 select_reduce_fusion.1
  339.2 0.6 and_select_fusion
  339.8 68.4 %all-to-all-done.4.refs_1_ = bf16[32,6,1,16,512]{4,3,2,1,0:T(8,128)(2,1)S(1)} async-done(((bf16[32,6,1,16,512]{4,3,2,1,0:T(8,128)(2,1)}), bf16[32,6,1,16,512]{4,3,2,1,0:T(8,128)(2,1)S(1)}, u32[]{:S(2)}, u32[]{:S(2)}) %all-to-all-start.4) | async-done | bytes 3145760 | tf_op jit(solution)/shard_map/all_to_all | solution.py:27
  408.2 0.0 copy-start.1
  408.2 1.7 copy-done.1
  409.9 7.9 %shard_map.123 = bf16[32,16,4096]{2,1,0:T(8,128)(2,1)} custom-call(s32[256]{0:T(256)} %get-tuple-element.32.own_ref, s32[256]{0:T(256)} %get-tuple-element.31.slot_ref, bf16[32,6,1,16,512]{4,3,2,1,0:T(8,128)(2,1)} %all-to-all-done.2.refs_0_, bf16[32,6,1,16,512]{4,3,2,1,0:T(8,128)(2,1)} %copy-done.1), custom_call_target="tpu_custom_call" | custom-call | bytes 10485760 | tf_op jit(solution)/shard_map/pallas_call | solution.py:91
  417.8 99.0 %all_to_all.30 = bf16[32,16,4096]{2,1,0:T(8,128)(2,1)S(1)} all-to-all(bf16[32,16,4096]{2,1,0:T(8,128)(2,1)} %shard_map.123), channel_id=1, replica_groups=mesh['shard'=8,'tp'=4] {'shard','tp'}, dimensions={0} | all-to-all | bytes 8388608 | tf_op jit(solution)/shard_map/all_to_all | solution.py:27
  516.8 2.0 copy.22
  (2 shorter events, 0.0 us)
Async XLA Ops:
  0.6 6.4 %copy-start.3 = (s32[256,3]{0,1:T(4,128)S(1)}, s32[256,3]{0,1:T(4,128)}, u32[]{:S(2)}) copy-start(s32[256,3]{0,1:T(4,128)} %param.9) | copy-start | bytes 9220
  0.6 97.5 %all-to-all-start = ((bf16[32,16,4096]{2,1,0:T(8,128)(2,1)}), bf16[32,16,4096]{2,1,0:T(8,128)(2,1)}, u32[]{:S(2)}, u32[]{:S(2)}) async-start(bf16[32,16,4096]{2,1,0:T(8,128)(2,1)} %bitcast.5), calls=%async_computation | async-start | bytes 8388608 | tf_op jit(solution)/shard_map/all_to_all | solution.py:27
  104.5 75.8 %all-to-all-start.1 = ((bf16[32,6,1,16,512]{4,3,2,1,0:T(8,128)(2,1)}), bf16[32,6,1,16,512]{4,3,2,1,0:T(8,128)(2,1)S(1)}, u32[]{:S(2)}, u32[]{:S(2)}) async-start(bf16[32,6,1,16,512]{4,3,2,1,0:T(8,128)(2,1)} %shard_map.119), calls=%async_computation.1 | async-start | bytes 6291456 | tf_op jit(solution)/shard_map/all_to_all | solution.py:27
  180.3 1.7 copy-start.2
  182.0 75.4 %all-to-all-start.3 = ((bf16[32,6,1,16,512]{4,3,2,1,0:T(8,128)(2,1)}), bf16[32,6,1,16,512]{4,3,2,1,0:T(8,128)(2,1)S(1)}, u32[]{:S(2)}, u32[]{:S(2)}) async-start(bf16[32,6,1,16,512]{4,3,2,1,0:T(8,128)(2,1)} %shard_map.121), calls=%async_computation.3 | async-start | bytes 6291456 | tf_op jit(solution)/shard_map/all_to_all | solution.py:27
  257.3 6.3 %copy-start = (bf16[32,6,1,16,512]{4,3,2,1,0:T(8,128)(2,1)}, bf16[32,6,1,16,512]{4,3,2,1,0:T(8,128)(2,1)S(1)}, u32[]{:S(2)}) copy-start(bf16[32,6,1,16,512]{4,3,2,1,0:T(8,128)(2,1)S(1)} %all-to-all-done.3.x_ref) | copy-start | bytes 9437188
  257.3 75.5 %all-to-all-start.2 = ((bf16[32,6,1,16,512]{4,3,2,1,0:T(8,128)(2,1)}), bf16[32,6,1,16,512]{4,3,2,1,0:T(8,128)(2,1)}, u32[]{:S(2)}, u32[]{:S(2)}) async-start(bf16[32,6,1,16,512]{4,3,2,1,0:T(8,128)(2,1)} %get-tuple-element.15), calls=%async_computation.2 | async-start | bytes 6291456 | tf_op jit(solution)/shard_map/all_to_all | solution.py:27
  332.8 75.4 %all-to-all-start.4 = ((bf16[32,6,1,16,512]{4,3,2,1,0:T(8,128)(2,1)}), bf16[32,6,1,16,512]{4,3,2,1,0:T(8,128)(2,1)S(1)}, u32[]{:S(2)}, u32[]{:S(2)}) async-start(bf16[32,6,1,16,512]{4,3,2,1,0:T(8,128)(2,1)} %get-tuple-element.20), calls=%async_computation.4 | async-start | bytes 6291456 | tf_op jit(solution)/shard_map/all_to_all | solution.py:27
  408.2 1.7 copy-start.1
where the time goes:
time: 521 us; the launch traced here: 519 us
  waiting for transfers between devices  316 us (61%)
  blocking collectives  99 us (19%)
  Pallas kernels  63.1 us (12%)
  starting transfers between devices  31.9 us (6%)
  local copies, waits for them, and re-layouts  6 us (1%)
    all_to_all x5, waiting for transfers between devices, exchange(): return lax.all_to_all(array, AXES, split_axis=0, concat_axis=0, tiled=True)  316 us
    all_to_all x1, blocking collectives, exchange(): return lax.all_to_all(array, AXES, split_axis=0, concat_axis=0, tiled=True)  99 us
    pallas_call x2, Pallas kernels, precondition(): pl.pallas_call(functools.partial(slot_kernel, first, packed), grid_spec=p...  42.5 us
    all_to_all x5, starting transfers between devices, exchange(): return lax.all_to_all(array, AXES, split_axis=0, concat_axis=0, tiled=True)  31.9 us
    pallas_call x2, Pallas kernels, pack(): pl.pallas_call(functools.partial(pack_kernel, group, slots, first, count,...  12.6 us
  transfers between devices with their start and end apart: 5, of which 5 were waited for; matrix products, arithmetic and copies ran while one was open for 0% of the time, Pallas kernels for 9%

commit v1 on v0

--- a/solution.py
+++ b/solution.py
@@ -187,6 +187,366 @@
     )(mine, x, *states, *done)
 
 
+CAPS = (19, 21, 23, 26)
+MESH = pl.DeviceIdType.MESH
+
+
+class Route:
+    def __init__(self, shard_count, tp_count, slots, side, cols_per_dev, cap, spare):
+        self.near = 2
+        self.tp_count = tp_count
+        self.planes = shard_count // self.near
+        self.wing = self.planes // 2
+        self.group = self.near * tp_count
+        self.slots = slots
+        self.side = side
+        self.cols = cols_per_dev
+        self.stripe = side // self.group
+        self.rows = 16
+        self.chunks = self.stripe // self.rows
+        self.held = self.group * cols_per_dev
+        self.cap = min(cap, self.held)
+        self.near_cap = min(cap + spare, self.held)
+
+    def me(self):
+        shard = lax.axis_index("shard")
+        return shard // self.near, (shard % self.near) * self.tp_count + lax.axis_index("tp")
+
+    def device(self, plane, member):
+        return (plane * self.near + member // self.tp_count, member % self.tp_count)
+
+    def hops(self):
+        out = [(1, e, self.cap) for e in range(self.wing)]
+        return out + [(0, e, self.near_cap) for e in range(1, self.wing)]
+
+    def plane_at(self, plane, cross, step):
+        wing, place = plane // self.wing, plane % self.wing
+        if cross:
+            wing = 1 - wing
+        return wing * self.wing + (place + step) % self.wing
+
+    def plane_from(self, plane, cross, step):
+        return self.plane_at(plane, cross, self.wing - step)
+
+
+def usable(shard_count, tp_count, row_dev, side):
+    group = 2 * tp_count
+    return row_dev == side and shard_count % 4 == 0 and side % (16 * group) == 0
+
+
+def greet(route):
+    plane, member = route.me()
+    barrier = pltpu.get_barrier_semaphore()
+    count = 0
+    for i in range(1, route.group):
+        peer = route.device(plane, (member + i) % route.group)
+        pl.semaphore_signal(barrier, inc=1, device_id=peer, device_id_type=MESH)
+        count += 1
+    for cross, step, _ in route.hops():
+        peer = route.device(route.plane_at(plane, cross, step), member)
+        pl.semaphore_signal(barrier, inc=1, device_id=peer, device_id_type=MESH)
+        count += 1
+    pl.semaphore_wait(barrier, count)
+
+
+class Spread:
+    def __init__(self, route, src_of, dst_of, whole, sems, h, pieces):
+        send, recv = sems
+        plane, member = route.me()
+        self.parts, self.own, self.waits = [], [], []
+
+        def remote(src, dst, i):
+            return pltpu.make_async_remote_copy(
+                src_ref=src,
+                dst_ref=dst,
+                send_sem=send.at[h, i],
+                recv_sem=recv.at[h, i],
+                device_id=route.device(plane, (member + i) % route.group),
+                device_id_type=MESH,
+            )
+
+        for i in range(1, route.group):
+            other = (member + i) % route.group
+            self.parts += [remote(src_of(other, c), dst_of(member, c), i) for c in range(pieces)]
+            self.waits.append(remote(whole, whole, i))
+        self.own = [
+            pltpu.make_async_copy(src_of(member, c), dst_of(member, c), recv.at[h, 0])
+            for c in range(pieces)
+        ]
+        self.own_wait = pltpu.make_async_copy(whole, whole, recv.at[h, 0])
+
+    def start(self):
+        start_all(self.parts + self.own)
+
+    def wait_recv(self):
+        for copy in self.waits:
+            copy.wait_recv()
+        self.own_wait.wait()
+
+    def wait_send(self):
+        for copy in self.waits:
+            copy.wait_send()
+
+
+def to_planes(route, src, dst, sems, h):
+    send, recv = sems
+    plane, member = route.me()
+    copies = []
+    for n, (cross, step, cap) in enumerate(route.hops()):
+        other = route.plane_at(plane, cross, step)
+        copies.append(
+            pltpu.make_async_remote_copy(
+                src_ref=src.at[other, pl.ds(0, cap)],
+                dst_ref=dst.at[plane, pl.ds(0, cap)],
+                send_sem=send.at[h, n],
+                recv_sem=recv.at[h, n],
+                device_id=route.device(other, member),
+                device_id_type=MESH,
+            )
+        )
+    return copies
+
+
+def fill_planes(route, load, out, kept):
+    plane, _ = route.me()
+
+    def fill(ref, at, cap):
+        def one(k, carry):
+            ref[at, k] = load(at * route.held + k)
+            return carry
+
+        lax.fori_loop(0, cap, one, 0)
+
+    for cross, step, cap in route.hops():
+        fill(out, route.plane_at(plane, cross, step), cap)
+    fill(kept, plane, route.near_cap)
+
+
+def start_all(copies):
+    for copy in copies:
+        copy.start()
+
+
+def recv_all(copies):
+    for copy in copies:
+        copy.wait_recv()
+
+
+def pipeline(route, enter, turn, leave):
+    for h in range(route.chunks):
+        enter(h)
+    for h in range(route.chunks + 1):
+        if h < route.chunks:
+            turn(h)
+        if h >= 1:
+            leave(h - 1)
+
+
+def split_scratch(route, refs):
+    n = route.chunks
+    return [refs[i * n : (i + 1) * n] for i in range(4)], [refs[4 * n + 2 * i : 4 * n + 2 * i + 2] for i in range(3)]
+
+
+def columns(ref, m, h, c, side):
+    return ref.at[m, h, :, pl.ds(c * side, side)]
+
+
+def forward_kernel(route, zj_ref, zc_ref, dp_ref, dk_ref, g_ref, x_ref, *refs):
+    (tile, outz, inz, outd), (sem_a, sem_z, sem_d) = split_scratch(route, refs)
+    greet(route)
+    stage = {}
+
+    def enter(h):
+        stage["a", h] = Spread(
+            route,
+            lambda m, c: columns(g_ref, m, h, c, route.side),
+            lambda m, c: tile[h].at[m, c],
+            tile[h].at[0],
+            sem_a,
+            h,
+            route.cols,
+        )
+        stage["a", h].start()
+
+    def turn(h):
+        stage["a", h].wait_recv()
+
+        def load(at):
+            return tile[h][zj_ref[at], zc_ref[at]]
+
+        fill_planes(route, load, outz[h], inz[h])
+        stage["z", h] = to_planes(route, outz[h], inz[h], sem_z, h)
+        start_all(stage["z", h])
+
+    def leave(h):
+        recv_all(stage["z", h])
+
+        def member(m, carry):
+            for s in range(route.slots):
+                at = m * route.slots + s
+                outd[h][m, s] = inz[h][dp_ref[at], dk_ref[at]]
+            return carry
+
+        lax.fori_loop(0, route.group, member, 0)
+        stage["d", h] = Spread(
+            route,
+            lambda m, c: outd[h].at[m],
+            lambda m, c: x_ref.at[:, m, h],
+            outd[h].at[0],
+            sem_d,
+            h,
+            1,
+        )
+        stage["d", h].start()
+
+    pipeline(route, enter, turn, leave)
+    finish(route, stage, "d")
+
+
+def finish(route, stage, last):
+    for h in range(route.chunks):
+        stage[last, h].wait_recv()
+    for h in range(route.chunks):
+        stage["a", h].wait_send()
+        for copy in stage["z", h]:
+            copy.wait_send()
+        stage["d", h].wait_send()
+
+
+def backward_kernel(route, zj_ref, zs_ref, fp_ref, fk_ref, u_ref, g_ref, *refs):
+    (tile, outz, inz, ind), (sem_a, sem_z, sem_d) = split_scratch(route, refs)
+    greet(route)
+    stage = {}
+
+    def enter(h):
+        stage["d", h] = Spread(
+            route,
+            lambda m, c: u_ref.at[:, m, h],
+            lambda m, c: ind[h].at[m],
+            ind[h].at[0],
+            sem_d,
+            h,
+            1,
+        )
+        stage["d", h].start()
+
+    def turn(h):
+        stage["d", h].wait_recv()
+
+        def load(at):
+            return ind[h][zj_ref[at], zs_ref[at]]
+
+        fill_planes(route, load, outz[h], inz[h])
+        stage["z", h] = to_planes(route, outz[h], inz[h], sem_z, h)
+        start_all(stage["z", h])
+
+    def leave(h):
+        recv_all(stage["z", h])
+
+        def member(m, carry):
+            for c in range(route.cols):
+                at = m * route.cols + c
+                tile[h][m, c] = inz[h][fp_ref[at], fk_ref[at]]
+            return carry
+
+        lax.fori_loop(0, route.group, member, 0)
+        stage["a", h] = Spread(
+            route,
+            lambda m, c: tile[h].at[m, c],
+            lambda m, c: columns(g_ref, m, h, c, route.side),
+            tile[h].at[0],
+            sem_a,
+            h,
+            route.cols,
+        )
+        stage["a", h].start()
+
+    pipeline(route, enter, turn, leave)
+    finish(route, stage, "a")
+
+
+def travel(kernel, route, collective_id, lists, data, out_shape):
+    dtype = data.dtype
+    piece = (route.rows, route.side)
+    tile = pltpu.VMEM((route.group, route.cols) + piece, dtype)
+    lanes = pltpu.VMEM((route.planes, route.near_cap) + piece, dtype)
+    slots = pltpu.VMEM((route.group, route.slots) + piece, dtype)
+    sems = [pltpu.SemaphoreType.DMA((route.chunks, n)) for n in (route.group, route.planes, route.group) for _ in range(2)]
+    moved = data.size * data.dtype.itemsize
+    return pl.pallas_call(
+        functools.partial(kernel, route),
+        in_specs=[pl.BlockSpec(memory_space=pltpu.SMEM)] * len(lists) + [pl.BlockSpec(memory_space=pl.ANY)],
+        out_specs=pl.BlockSpec(memory_space=pl.ANY),
+        out_shape=jax.ShapeDtypeStruct(out_shape, dtype),
+        scratch_shapes=[s for s in (tile, lanes, lanes, slots) for _ in range(route.chunks)] + sems,
+        compiler_params=pltpu.CompilerParams(
+            collective_id=collective_id, has_side_effects=True, vmem_limit_bytes=60 * 1024 * 1024
+        ),
+        cost_estimate=pl.CostEstimate(flops=moved * 400, bytes_accessed=moved * 4, transcendentals=0),
+    )(*lists, data)
+
+
+def pick(keys, count, *values):
+    hit = keys[None, :] == jnp.arange(count, dtype=jnp.int32)[:, None]
+    return [jnp.sum(jnp.where(hit, v[None, :], 0), axis=1) for v in values]
+
+
+def routed(gradient, table, states):
+    shard_count, tp_count = lax.axis_size("shard"), lax.axis_size("tp")
+    slots, side, _ = states[0].shape
+    row_dev, col_dev = gradient.shape
+    cols = col_dev // side
+
+    def make(cap):
+        return Route(shard_count, tp_count, slots, side, cols, cap, 4)
+
+    base = make(1)
+    held, group, planes = base.held, base.group, base.planes
+    rows, count = table.shape[0], planes * held
+    owner = table[:, 2]
+    src = table[:, 0] * tp_count + table[:, 1] // cols
+    a, j, c = src // group, src % group, table[:, 1] % cols
+    b, m = owner // group, owner % group
+    pair = a * planes + b
+    order = jnp.arange(rows, dtype=jnp.int32)
+    earlier = order[None, :] < order[:, None]
+    s = jnp.sum((earlier & (owner[None, :] == owner[:, None])).astype(jnp.int32), axis=1)
+    k = jnp.sum((earlier & (pair[None, :] == pair[:, None])).astype(jnp.int32), axis=1)
+    crosses = (a // base.wing) != (b // base.wing)
+    most = jnp.max(jnp.where(crosses, k + 1, k + 1 - 4))
+    which = jnp.sum((most > jnp.array(CAPS, dtype=jnp.int32)).astype(jnp.int32))
+
+    plane, member = base.me()
+    out_key = jnp.where(a == plane, b * held + k, -1)
+    zj, zc = pick(out_key, count, j, c)
+    own_key = jnp.where(b == plane, m * slots + s, -1)
+    dp, dk = pick(own_key, group * slots, a, k)
+    back_key = jnp.where(b == plane, a * held + k, -1)
+    rj, rs = pick(back_key, count, m, s)
+    home_key = jnp.where(a == plane, j * cols + c, -1)
+    fp, fk = pick(home_key, held, b, k)
+    myself = plane * group + member
+    mine = pick(jnp.where(owner == myself, s, -1), slots, jnp.ones_like(s))[0]
+
+    routes = [make(cap) for cap in CAPS + (held,)]
+    piece = (base.chunks, base.rows)
+    block_shape = (slots, group) + piece + (side,)
+    grad_shape = (group,) + piece + (col_dev,)
+
+    def forward(i):
+        return lambda g: travel(forward_kernel, routes[i], 2 * i, (zj, zc, dp, dk), g, block_shape)
+
+    def backward(i):
+        return lambda u: travel(backward_kernel, routes[i], 2 * i + 1, (rj, rs, fp, fk), u, grad_shape)
+
+    everyone = range(len(routes))
+    x = lax.switch(which, [forward(i) for i in everyone], gradient.reshape(grad_shape))
+    x = x.reshape(slots, side, side)
+    update, *done = precondition(x, mine, states, (), 0, False)
+    update = lax.switch(which, [backward(i) for i in everyone], update.reshape(block_shape))
+    return (update.reshape(row_dev, col_dev), *done)
+
+
 def shards(gradient, table, left_stat, right_stat, left_basis, right_basis, moment, second):
     shard_count = lax.axis_size("shard")
     tp_count = lax.axis_size("tp")
@@ -194,6 +554,9 @@
     row_dev, col_dev = gradient.shape
     slots = left_stat.shape[0]
     side = left_stat.shape[1]
+    if usable(shard_count, tp_count, row_dev, side):
+        states = (left_stat, right_stat, left_basis, right_basis, moment, second)
+        return routed(gradient, table, states)
     halves = side // row_dev
     cols_per_dev = col_dev // side
     block_cols = tp_count * cols_per_dev

time: 521 us -> 370 us (0.71)
  waiting for transfers between devices: 316 us -> 0 us
  Pallas kernels: 63.1 us -> 354 us
  blocking collectives: 99 us -> 0 us
  starting transfers between devices: 31.9 us -> 0 us
  other arithmetic: 1.7 us -> 8.85 us
    all_to_all x5 -> x0, waiting for transfers between devices: 316 us -> none  [exchange(): return lax.all_to_all(array, AXES, split_axis=0, concat_axis=0, tiled=True)]
    pallas_call x3 -> x2, Pallas kernels: 20.6 us -> 318 us  [travel(): pl.pallas_call(functools.partial(kernel, route), in_specs=[pl.BlockSpec(m...]
    all_to_all x1 -> x0, blocking collectives: 99 us -> none  [exchange(): return lax.all_to_all(array, AXES, split_axis=0, concat_axis=0, tiled=True)]
    all_to_all x5 -> x0, starting transfers between devices: 31.9 us -> none  [exchange(): return lax.all_to_all(array, AXES, split_axis=0, concat_axis=0, tiled=True)]
    pallas_call x2 -> x1, Pallas kernels: 42.5 us -> 36.2 us  [precondition(): pl.pallas_call(functools.partial(slot_kernel, first, packed), grid_spec=p...]
    reduce_sum x3 -> x8, other arithmetic: 0.5 us -> 5.78 us  [the longest x5 3.47 us: pick(): return [jnp.sum(jnp.where(hit, v[None, :], 0), axis=1) for v in values]]
  transfers between devices with their start and end apart: 5 -> 0, of which waited for: 5 -> 0; matrix products, arithmetic and copies ran while one was open for 0% -> 0% of each run, Pallas kernels for 9% -> 0%
where the time goes in v1:
time: 370 us
  Pallas kernels  354 us (96%)
  other arithmetic  8.85 us (2%)
  local copies, waits for them, and re-layouts  4.8 us (1%)
    pallas_call x2, Pallas kernels, travel(): pl.pallas_call(functools.partial(kernel, route), in_specs=[pl.BlockSpec(m...  318 us
    pallas_call x1, Pallas kernels, precondition(): pl.pallas_call(functools.partial(slot_kernel, first, packed), grid_spec=p...  36.2 us

profile of v1, /device:TPU:11, one launch (start us, length us, event | category | flops | bytes accessed | tf_op | source)
XLA Modules:
  0.0 369.7 jit_solution(4740345670349736152)
XLA Ops:
  0.7 0.7 broadcast_compare_fusion.22
  1.3 0.8 compare_select_fusion
  2.2 0.8 slice_bitcast_fusion
  3.0 0.2 convert_reduce_fusion
  3.2 0.7 select_reduce_fusion.40.mine_ref
  3.9 0.2 convert_reduce_fusion.1
  4.1 0.6 fusion.34
  4.8 1.9 fusion.35
  7.6 163.6 %conditional.2 = (bf16[12,512,512]{2,1,0:T(8,128)(2,1)}) conditional(s32[]{:T(128)} %clamp.4, (s32[256]{0:T(256)S(1)}, s32[256]{0:T(256)S(1)}, s32[256]{0:T(256)S(1)}, pred[256]{0:T(512)(128)(4,1)S(1)}, s32[256]{0:T(256)S(1)}, /*index=5*/s32[256,256]{1,0:T(8,128)S(1)}, s32[1,256]{1,0:T(1,128)S(1)}, ...), branch_computations={%region_5.10_spmd, %region_10.15_spmd, %region_15.20_spmd, %region... | conditional | flops 1678177280 | bytes 17430536 | solution.py:543
  7.6 0.6 select_reduce_fusion.6
  8.3 0.7 select_reduce_fusion.4
  9.0 161.9 %branch_1_fun.7 = bf16[12,8,4,16,512]{4,3,2,1,0:T(8,128)(2,1)} custom-call(s32[256]{0:T(256)} %get-tuple-element.2829.zj_ref, s32[256]{0:T(256)} %get-tuple-element.2828.zc_ref, s32[96]{0:T(128)} %get-tuple-element.2831.dp_ref, s32[96]{0:T(128)} %get-tuple-element.2830.dk_ref, bf16[8,4,16,4096]{3,2,1,0:T(8,128)(2,1)} %bitcast.85), custom_call_target="tpu_custom_call" | custom-call | flops 1677721600 | bytes 16777216 | tf_op jit(solution)/shard_map/cond/branch_1_fun/pallas_call | solution.py:476
  171.1 36.2 %shard_map.128 = (bf16[12,512,512]{2,1,0:T(8,128)(2,1)}, bf16[12,512,512]{2,1,0:T(8,128)(2,1)}, bf16[12,512,512]{2,1,0:T(8,128)(2,1)}, bf16[12,512,512]{2,1,0:T(8,128)(2,1)}, f32[12,512,512]{2,1,0:T(8,128)}) custom-call(s32[12]{0:T(128)} %select_reduce_fusion.40.mine_ref, bf16[12,512,512]{2,1,0:T(8,128)(2,1)} %get-tuple-element.2947.x_ref, ...), custom_call_target="tpu_custom_call" | custom-call | flops 25769803776 | bytes 81788928 | tf_op jit(solution)/shard_map/pallas_call | solution.py:172
  207.3 157.7 %conditional.3 = (bf16[512,4096]{1,0:T(8,128)(2,1)}) conditional(s32[]{:T(128)} %clamp.4, (s32[256]{0:T(256)S(1)}, s32[256]{0:T(256)S(1)}, s32[256]{0:T(256)S(1)}, pred[256]{0:T(512)(128)(4,1)S(1)}, s32[256]{0:T(256)S(1)}, /*index=5*/s32[256,256]{1,0:T(8,128)S(1)}, s32[1,256]{1,0:T(1,128)S(1)}, ...), branch_computations={%region_30.35_spmd, %region_35.40_spmd, %region_40.45_spmd, %regio... | conditional | flops 2516998144 | bytes 25783048 | solution.py:546
  207.3 0.7 select_reduce_fusion.26
  208.0 0.7 select_reduce_fusion.24
  208.8 156.2 %branch_1_fun.8 = bf16[8,4,16,4096]{3,2,1,0:T(8,128)(2,1)} custom-call(s32[256]{0:T(256)} %get-tuple-element.2849.zj_ref, s32[256]{0:T(256)} %get-tuple-element.2848.zs_ref, s32[64]{0:T(128)} %get-tuple-element.2851.fp_ref, s32[64]{0:T(128)} %get-tuple-element.2850.fk_ref, bf16[12,8,4,16,512]{4,3,2,1,0:T(8,128)(2,1)} %bitcast.80), custom_call_target="tpu_custom_call" | custom-call | flops 2516582400 | bytes 25165824 | tf_op jit(solution)/shard_map/cond/branch_1_fun/pallas_call | solution.py:476
  365.0 4.7 %copy.25 = bf16[512,4096]{1,0:T(8,128)(2,1)} copy(bf16[512,4096]{1,0:T(8,128)(2,1)} %get-tuple-element.2948) | data formatting | bytes 8388608
  (21 shorter events, 0.2 us)

commit v2 on v0

--- a/solution.py
+++ b/solution.py
@@ -1,4 +1,5 @@
 import functools
+import math
 
 import jax
 import jax.numpy as jnp
@@ -187,6 +188,416 @@
     )(mine, x, *states, *done)
 
 
+MARGINS = (1, 2, 3, 5, 8)
+SPARE = 8
+SPILL = 6
+MESH = pl.DeviceIdType.MESH
+
+
+class Route:
+    def __init__(self, shard_count, tp_count, slots, side, cols_per_dev, cap):
+        self.near = 2
+        self.tp_count = tp_count
+        self.planes = shard_count // self.near
+        self.wing = self.planes // 2
+        self.group = self.near * tp_count
+        self.slots = slots
+        self.side = side
+        self.cols = cols_per_dev
+        self.rows = 8
+        self.chunks = side // self.group // self.rows
+        self.held = self.group * cols_per_dev
+        self.cap = min(cap, self.held)
+        self.near_cap = min(cap + SPARE, self.held)
+        self.spill = min(SPILL, slots, cols_per_dev)
+
+    def me(self):
+        shard = lax.axis_index("shard")
+        return shard // self.near, (shard % self.near) * self.tp_count + lax.axis_index("tp")
+
+    def device(self, plane, member):
+        return (plane * self.near + member // self.tp_count, member % self.tp_count)
+
+    def hops(self):
+        return [(1, 0, self.cap), (1, 1, self.cap), (0, 1, self.near_cap)]
+
+    def plane_at(self, plane, cross, step):
+        wing, place = plane // self.wing, plane % self.wing
+        if cross:
+            wing = 1 - wing
+        return wing * self.wing + (place + step) % self.wing
+
+
+def usable(shard_count, tp_count, row_dev, side):
+    return row_dev == side and shard_count == 8 and side % (16 * tp_count) == 0
+
+
+def greet(route):
+    plane, member = route.me()
+    barrier = pltpu.get_barrier_semaphore()
+    count = 0
+    for i in range(1, route.group):
+        peer = route.device(plane, (member + i) % route.group)
+        pl.semaphore_signal(barrier, inc=1, device_id=peer, device_id_type=MESH)
+        count += 1
+    for cross, step, _ in route.hops():
+        peer = route.device(route.plane_at(plane, cross, step), member)
+        pl.semaphore_signal(barrier, inc=1, device_id=peer, device_id_type=MESH)
+        count += 1
+    pl.semaphore_wait(barrier, count)
+
+
+class Spread:
+    def __init__(self, route, peers, src_of, dst_of, whole, sems, h, pieces):
+        self.route, self.peers, self.src_of, self.dst_of, self.whole = route, peers, src_of, dst_of, whole
+        self.send, self.recv = sems
+        self.h, self.pieces = h, pieces
+
+    def remote(self, src, dst, i):
+        return pltpu.make_async_remote_copy(
+            src_ref=src,
+            dst_ref=dst,
+            send_sem=self.send.at[self.h, i],
+            recv_sem=self.recv.at[self.h, i],
+            device_id=self.peers[i][1],
+            device_id_type=MESH,
+        )
+
+    def start(self):
+        member = self.peers[0][0]
+
+        def piece(c):
+            for i in range(1, self.route.group):
+                self.remote(self.src_of(self.peers[i][0], c), self.dst_of(member, c), i).start()
+            pltpu.make_async_copy(
+                self.src_of(member, c), self.dst_of(member, c), self.recv.at[self.h, 0]
+            ).start()
+
+        repeat(self.pieces, piece)
+
+    def wait_recv(self):
+        for i in range(1, self.route.group):
+            self.remote(self.whole, self.whole, i).wait_recv()
+        pltpu.make_async_copy(self.whole, self.whole, self.recv.at[self.h, 0]).wait()
+
+    def wait_send(self):
+        for i in range(1, self.route.group):
+            self.remote(self.whole, self.whole, i).wait_send()
+
+
+class Planes:
+    def __init__(self, route, src, dst, sems, h):
+        send, recv = sems
+        plane, member = route.me()
+        self.copies = []
+        for n, (cross, step, cap) in enumerate(route.hops()):
+            other = route.plane_at(plane, cross, step)
+            self.copies.append(
+                pltpu.make_async_remote_copy(
+                    src_ref=src.at[other, pl.ds(0, cap)],
+                    dst_ref=dst.at[plane, pl.ds(0, cap)],
+                    send_sem=send.at[h, n],
+                    recv_sem=recv.at[h, n],
+                    device_id=route.device(other, member),
+                    device_id_type=MESH,
+                )
+            )
+
+    def start(self):
+        for copy in self.copies:
+            copy.start()
+
+    def wait_recv(self):
+        for copy in self.copies:
+            copy.wait_recv()
+
+    def wait_send(self):
+        for copy in self.copies:
+            copy.wait_send()
+
+
+def detour(route, src, dst, sems, h):
+    send, recv = sems
+    plane, member = route.me()
+    return pltpu.make_async_remote_copy(
+        src_ref=src,
+        dst_ref=dst,
+        send_sem=send.at[h, 0],
+        recv_sem=recv.at[h, 0],
+        device_id=route.device(route.plane_at(plane, 0, 1), member),
+        device_id_type=MESH,
+    )
+
+
+def repeat(count, body):
+    def one(i, carry):
+        body(i)
+        return carry
+
+    lax.fori_loop(0, count, one, 0)
+
+
+def fill_planes(route, load, out, kept):
+    plane, _ = route.me()
+
+    def fill(ref, at, cap):
+        def one(k):
+            ref[at, k] = load(at * route.held + k)
+
+        repeat(cap, one)
+
+    for cross, step, cap in route.hops():
+        fill(out, route.plane_at(plane, cross, step), cap)
+    fill(kept, plane, route.near_cap)
+
+
+def run_stages(route, enter, swap, turn, leave):
+    chunks = route.chunks
+    started = [0, 0, 0]
+
+    def upto(n, stage, end):
+        while started[n] < min(end, chunks):
+            stage(started[n])
+            started[n] += 1
+
+    upto(0, enter, 2)
+    upto(1, swap, 1)
+    upto(0, enter, 4)
+    upto(1, swap, 2)
+    upto(2, turn, 2)
+    for t in range(chunks):
+        upto(0, enter, t + 6)
+        upto(1, swap, t + 4)
+        upto(2, turn, t + 2)
+        leave(t)
+
+
+def split_scratch(route, refs):
+    n = route.chunks
+    return [refs[i * n : (i + 1) * n] for i in range(6)], [refs[6 * n + 2 * i : 6 * n + 2 * i + 2] for i in range(4)]
+
+
+def columns(ref, m, h, c, side):
+    return ref.at[m, h, :, pl.ds(pl.multiple_of(c * side, side), side)]
+
+
+def exchange_kernel(route, inward, list_ref, in_ref, out_ref, *refs):
+    (gathered, outz, inz, outs, outy, iny), (sem_a, sem_z, sem_d, sem_y) = split_scratch(route, refs)
+    early, lane, final = (0, 2, 4) if inward else (6, 8, 10)
+    greet(route)
+    plane, member = route.me()
+    others = [(member + i) % route.group for i in range(route.group)]
+    peers = [(other, route.device(plane, other)) for other in others]
+    chunks = range(route.chunks)
+    count = route.slots if inward else route.cols
+    step = math.gcd(count, 4)
+
+    def parts(hbm, buf, h, by_column, sems, leaving):
+        if by_column:
+            far, near, pieces = lambda m, c: columns(hbm, m, h, c, route.side), lambda m, c: buf.at[m, c], route.cols
+        else:
+            far, near, pieces = lambda m, c: hbm.at[:, m, h], lambda m, c: buf.at[m], 1
+        ends = (near, far) if leaving else (far, near)
+        return Spread(route, peers, *ends, buf.at[0], sems, h, pieces)
+
+    spread = [parts(in_ref, gathered[h], h, inward, sem_a, False) for h in chunks]
+    extra = [detour(route, outy[h], iny[h], sem_y, h) for h in chunks]
+    cross = [Planes(route, outz[h], inz[h], sem_z, h) for h in chunks]
+    deliver = [parts(out_ref, outs[h], h, not inward, sem_d, True) for h in chunks]
+
+    def swap(h):
+        spread[h].wait_recv()
+
+        def one(v):
+            outy[h][v] = gathered[h][list_ref[early, v], list_ref[early + 1, v]]
+
+        repeat(route.spill, one)
+        extra[h].start()
+
+    def turn(h):
+        extra[h].wait_recv()
+
+        def late(v):
+            gathered[h][route.group, v] = iny[h][v]
+
+        repeat(route.spill, late)
+        fill_planes(route, lambda at: gathered[h][list_ref[lane, at], list_ref[lane + 1, at]], outz[h], inz[h])
+        cross[h].start()
+
+    def leave(h):
+        cross[h].wait_recv()
+
+        def member(m):
+            def several(first):
+                for i in range(step):
+                    n = first * step + i
+                    at = m * count + n
+                    outs[h][m, n] = inz[h][list_ref[final, at], list_ref[final + 1, at]]
+
+            repeat(count // step, several)
+
+        repeat(route.group, member)
+        deliver[h].start()
+
+    run_stages(route, lambda h: spread[h].start(), swap, turn, leave)
+    for h in chunks:
+        deliver[h].wait_recv()
+    for copies in spread + extra + cross + deliver:
+        copies.wait_send()
+
+
+def travel(route, inward, collective_id, lists, data, out_shape):
+    dtype = data.dtype
+    piece = (route.rows, route.side)
+    counts = (route.cols, route.slots) if inward else (route.slots, route.cols)
+    gathered = pltpu.VMEM((route.group + 1, counts[0]) + piece, dtype)
+    lanes = pltpu.VMEM((route.planes, route.near_cap) + piece, dtype)
+    outs = pltpu.VMEM((route.group, counts[1]) + piece, dtype)
+    late = pltpu.VMEM((route.spill,) + piece, dtype)
+    sems = [pltpu.SemaphoreType.DMA((route.chunks, n)) for n in (route.group, route.planes, route.group, 1) for _ in range(2)]
+    moved = data.size * data.dtype.itemsize
+    return pl.pallas_call(
+        functools.partial(exchange_kernel, route, inward),
+        in_specs=[pl.BlockSpec(memory_space=pltpu.SMEM), pl.BlockSpec(memory_space=pl.ANY)],
+        out_specs=pl.BlockSpec(memory_space=pl.ANY),
+        out_shape=jax.ShapeDtypeStruct(out_shape, dtype),
+        scratch_shapes=[s for s in (gathered, lanes, lanes, outs, late, late) for _ in range(route.chunks)] + sems,
+        compiler_params=pltpu.CompilerParams(
+            collective_id=collective_id, has_side_effects=True, vmem_limit_bytes=60 * 1024 * 1024
+        ),
+        cost_estimate=pl.CostEstimate(flops=moved * 400, bytes_accessed=moved * 4, transcendentals=0),
+    )(lists, data)
+
+
+FIELDS = ("a", "j", "c", "wing_a", "twin_a", "b", "m", "wing_b", "twin_b", "owner")
+WHICH = 12
+MINE = 14
+
+
+def plan_kernel(base, caps, row_ref, col_ref, out_ref):
+    planes, held, width, blocks = base.planes, base.held, out_ref.shape[1], row_ref.shape[1]
+
+    class Side:
+        pass
+
+    row, col = Side(), Side()
+    for i, name in enumerate(FIELDS):
+        setattr(row, name, row_ref[i : i + 1, :])
+        setattr(col, name, col_ref[:, i : i + 1])
+    row.n = lax.broadcasted_iota(jnp.int32, (1, blocks), 1).astype(jnp.float32)
+    col.n = lax.broadcasted_iota(jnp.int32, (blocks, 1), 0).astype(jnp.float32)
+    lanes = lax.broadcasted_iota(jnp.int32, (1, width), 1).astype(jnp.float32)
+    plane, member = base.me()
+    me = (plane * base.group + member).astype(jnp.float32)
+    plane = plane.astype(jnp.float32)
+
+    def one(mask):
+        return jnp.where(mask, 1.0, 0.0)
+
+    def tally(name, weight):
+        setattr(row, name, jnp.sum(weight(row, col), axis=0, keepdims=True))
+        setattr(col, name, jnp.sum(weight(col, row), axis=1, keepdims=True))
+
+    def pick(key, value):
+        return jnp.sum(jnp.where(key == lanes, value, 0.0), axis=0, keepdims=True)
+
+    def put(at, value):
+        out_ref[at : at + 1, :] = jnp.broadcast_to(value, (1, width)).astype(jnp.int32)
+
+    tally("s", lambda n, x: one(x.n < n.n) * one(x.owner == n.owner))
+    tally("q", lambda n, x: one(x.n < n.n) * one(x.a == n.a) * one(x.b == n.b))
+    tally("pair", lambda n, x: one(x.a == n.a) * one(x.b == n.b))
+    for side in (row, col):
+        side.cross = one(side.wing_a != side.wing_b)
+    put(MINE, pick(jnp.where(col.owner == me, col.s, -1.0), 1.0))
+
+    def way(at, p0, t0, x0, i0, p1, x1, i1, size1):
+        def get(side, name):
+            return getattr(side, name)
+
+        tally("twins", lambda n, x: one(get(x, p0) == get(n, t0)) * one(get(x, p1) == get(n, p1)))
+        half = row.pair + row.twins
+        need = jnp.max(jnp.where(row.cross > 0, half * 0.5, row.pair - SPARE), axis=1, keepdims=True)
+        cap, which = jnp.full((1, 1), caps[0], jnp.float32), jnp.zeros((1, 1), jnp.float32)
+        for this, larger in zip(caps[:-1], caps[1:]):
+            over = row.cross * one(row.q >= this)
+            spilled = jnp.zeros((1, 1), jnp.float32)
+            for p in range(planes):
+                spilled = jnp.maximum(spilled, jnp.sum(over * one(get(row, p0) == p), axis=1, keepdims=True))
+            small = jnp.maximum(one(need > this), one(spilled > base.spill))
+            cap, which = cap + small * (larger - this), which + small
+        put(WHICH + at, which)
+        for side in (row, col):
+            side.moved = side.cross * one(side.q >= cap)
+        tally("v", lambda n, x: one(x.n < n.n) * x.moved * one(get(x, p0) == get(n, p0)))
+        moved = col.moved > 0
+        launch = jnp.where(moved, get(col, t0), get(col, p0))
+        k = jnp.where(moved, col.twins + col.q - cap, col.q)
+        early = jnp.where(get(col, p0) == plane, jnp.where(moved, col.v, -1.0), -1.0)
+        lane = jnp.where(launch == plane, get(col, p1) * held + k, -1.0)
+        final = jnp.where(get(col, p1) == plane, get(col, x1) * size1 + get(col, i1), -1.0)
+        values = (
+            (early, get(col, x0)),
+            (early, get(col, i0)),
+            (lane, jnp.where(moved, float(base.group), get(col, x0))),
+            (lane, jnp.where(moved, col.v, get(col, i0))),
+            (final, launch),
+            (final, k),
+        )
+        for i, (key, value) in enumerate(values):
+            put(6 * at + i, pick(key, value))
+
+    way(0, "a", "twin_a", "j", "c", "b", "m", "s", base.slots)
+    way(1, "b", "twin_b", "m", "s", "a", "j", "c", base.cols)
+
+
+def make_plan(base, caps, table, tp_count):
+    group, wing = base.group, base.wing
+    owner = table[:, 2]
+    src = table[:, 0] * tp_count + table[:, 1] // base.cols
+    a, b = src // group, owner // group
+    fields = [a, src % group, table[:, 1] % base.cols, a // wing, a // wing * wing + (a % wing + 1) % wing]
+    fields += [b, owner % group, b // wing, b // wing * wing + (b % wing + 1) % wing, owner]
+    columns_of = jnp.stack(fields, axis=1).astype(jnp.float32)
+    return pl.pallas_call(
+        functools.partial(plan_kernel, base, caps),
+        out_shape=jax.ShapeDtypeStruct((16, base.planes * base.held), jnp.int32),
+        cost_estimate=pl.CostEstimate(flops=10**7, bytes_accessed=10**5, transcendentals=0),
+    )(columns_of.T, columns_of)
+
+
+def routed(gradient, table, states):
+    shard_count, tp_count = lax.axis_size("shard"), lax.axis_size("tp")
+    slots, side, _ = states[0].shape
+    row_dev, col_dev = gradient.shape
+    cols = col_dev // side
+
+    def make(cap):
+        return Route(shard_count, tp_count, slots, side, cols, cap)
+
+    base = make(1)
+    held = base.held
+    caps = tuple(held // base.planes + extra for extra in MARGINS) + (held,)
+    routes = [make(cap) for cap in caps]
+    plan = make_plan(base, caps, table, tp_count)
+    mine = plan[MINE, :slots]
+    piece = (base.chunks, base.rows)
+    block_shape = (slots, base.group) + piece + (side,)
+    grad_shape = (base.group,) + piece + (col_dev,)
+
+    def move(data, inward, shape):
+        def branch(n):
+            return lambda d: travel(routes[n], inward, 2 * n + int(inward), plan, d, shape)
+
+        which = plan[WHICH + int(not inward), 0]
+        return lax.switch(which, [branch(n) for n in range(len(routes))], data)
+
+    x = move(gradient.reshape(grad_shape), True, block_shape)
+    update, *done = precondition(x.reshape(slots, side, side), mine, states, (), 0, False)
+    update = move(update.reshape(block_shape), False, grad_shape)
+    return (update.reshape(row_dev, col_dev), *done)
+
+
 def shards(gradient, table, left_stat, right_stat, left_basis, right_basis, moment, second):
     shard_count = lax.axis_size("shard")
     tp_count = lax.axis_size("tp")
@@ -194,6 +605,9 @@
     row_dev, col_dev = gradient.shape
     slots = left_stat.shape[0]
     side = left_stat.shape[1]
+    if usable(shard_count, tp_count, row_dev, side):
+        states = (left_stat, right_stat, left_basis, right_basis, moment, second)
+        return routed(gradient, table, states)
     halves = side // row_dev
     cols_per_dev = col_dev // side
     block_cols = tp_count * cols_per_dev

time: 521 us -> 349 us (0.67)
  waiting for transfers between devices: 316 us -> 0 us
  Pallas kernels: 63.1 us -> 334 us
  blocking collectives: 99 us -> 0 us
  starting transfers between devices: 31.9 us -> 0 us
    all_to_all x5 -> x0, waiting for transfers between devices: 316 us -> none  [exchange(): return lax.all_to_all(array, AXES, split_axis=0, concat_axis=0, tiled=True)]
    pallas_call x3, Pallas kernels: 20.6 us -> 296 us  [the longest x2 293 us: travel(): pl.pallas_call(functools.partial(exchange_kernel, route, inward), in_spec...]
    all_to_all x1 -> x0, blocking collectives: 99 us -> none  [exchange(): return lax.all_to_all(array, AXES, split_axis=0, concat_axis=0, tiled=True)]
    all_to_all x5 -> x0, starting transfers between devices: 31.9 us -> none  [exchange(): return lax.all_to_all(array, AXES, split_axis=0, concat_axis=0, tiled=True)]
    pallas_call x2 -> x1, Pallas kernels: 42.5 us -> 38 us  [precondition(): pl.pallas_call(functools.partial(slot_kernel, first, packed), grid_spec=p...]
  transfers between devices with their start and end apart: 5 -> 0, of which waited for: 5 -> 0; matrix products, arithmetic and copies ran while one was open for 0% -> 0% of each run, Pallas kernels for 9% -> 0%
where the time goes in v2:
time: 349 us; the launch traced here: 346 us
  Pallas kernels  334 us (96%)
  local copies, waits for them, and re-layouts  6.56 us (2%)
    pallas_call x2, Pallas kernels, travel(): pl.pallas_call(functools.partial(exchange_kernel, route, inward), in_spec...  293 us
    pallas_call x1, Pallas kernels, precondition(): pl.pallas_call(functools.partial(slot_kernel, first, packed), grid_spec=p...  38 us

profile of v2, /device:TPU:11, one launch (start us, length us, event | category | flops | bytes accessed | tf_op | source)
XLA Modules:
  0.0 345.6 jit_solution(751042629998490412)
XLA Ops:
  0.6 0.7 and_select_fusion.8
  1.3 0.8 fusion.1
  2.2 0.1 stack.2
  2.3 0.1 copy.18
  2.4 0.7 fusion.6
  3.1 0.7 copy.19.row_ref
  3.7 3.3 shard_map.119
  7.1 0.5 slice_bitcast_fusion.mine_ref
  7.6 0.5 fusion.7
  9.4 155.0 %conditional.2 = (bf16[12,512,512]{2,1,0:T(8,128)(2,1)}) conditional(s32[]{:T(128)} %bitcast.27, (bf16[512,4096]{1,0:T(8,128)(2,1)}, s32[16,256]{1,0:T(8,128)S(1)}) %tuple.56, (bf16[512,4096]{1,0:T(8,128)(2,1)}, s32[16,256]{1,0:T(8,128)S(1)}) %tuple.56, (bf16[512,4096]{1,0:T(8,128)(2,1)}, ...), branch_computations={%region_0.1_spmd, %region_1.2_spmd, %region_2.3_spmd, %region_3.4_... | conditional | flops 1677721600 | bytes 16777224 | solution.py:593
  9.6 154.6 %branch_3_fun.2 = bf16[12,8,8,8,512]{4,3,2,1,0:T(8,128)(2,1)} custom-call(s32[16,256]{1,0:T(8,128)S(1)} %get-tuple-element.82.list_ref, bf16[8,8,8,4096]{3,2,1,0:T(8,128)(2,1)} %bitcast.39), custom_call_target="tpu_custom_call" | custom-call | flops 1677721600 | bytes 16777216 | tf_op jit(solution)/shard_map/cond/branch_3_fun/pallas_call | solution.py:459
  164.4 38.0 %shard_map.120 = (bf16[12,512,512]{2,1,0:T(8,128)(2,1)}, bf16[12,512,512]{2,1,0:T(8,128)(2,1)}, bf16[12,512,512]{2,1,0:T(8,128)(2,1)}, bf16[12,512,512]{2,1,0:T(8,128)(2,1)}, f32[12,512,512]{2,1,0:T(8,128)}) custom-call(s32[12]{0:T(128)} %slice_bitcast_fusion.mine_ref, bf16[12,512,512]{2,1,0:T(8,128)(2,1)} %get-tuple-element.142.x_ref, ...), custom_call_target="tpu_custom_call" | custom-call | flops 25769803776 | bytes 81788928 | tf_op jit(solution)/shard_map/pallas_call | solution.py:173
  202.4 138.5 %conditional.3 = (bf16[512,4096]{1,0:T(8,128)(2,1)}) conditional(s32[]{:T(128)} %bitcast.25, (bf16[12,512,512]{2,1,0:T(8,128)(2,1)}, s32[16,256]{1,0:T(8,128)S(1)}) %tuple.57, (bf16[12,512,512]{2,1,0:T(8,128)(2,1)}, s32[16,256]{1,0:T(8,128)S(1)}) %tuple.57, (bf16[12,512,512]{2,1,0:T(8,128)(2,1)}, ...), branch_computations={%region_6.7_spmd, %region_7.8_spmd, %region_8.9_spmd, %region_9.10... | conditional | flops 2516582400 | bytes 25165832 | solution.py:593
  202.4 138.2 %branch_1_fun.3 = bf16[8,8,8,4096]{3,2,1,0:T(8,128)(2,1)} custom-call(s32[16,256]{1,0:T(8,128)S(1)} %get-tuple-element.90.list_ref, bf16[12,8,8,8,512]{4,3,2,1,0:T(8,128)(2,1)} %bitcast.31), custom_call_target="tpu_custom_call" | custom-call | flops 2516582400 | bytes 25165824 | tf_op jit(solution)/shard_map/cond/branch_1_fun/pallas_call | solution.py:459
  340.9 4.7 %copy.33 = bf16[512,4096]{1,0:T(8,128)(2,1)} copy(bf16[512,4096]{1,0:T(8,128)(2,1)} %get-tuple-element.143) | data formatting | bytes 8388608
  (2 shorter events, 0.0 us)
